TPU v7x, 32 devices: a whole 2x2x4 slice. The times are simulated.
32 devices in a mesh: dp: 2 (over core), row: 4 (over y, x), col: 4 (over z).
Axes of the slice: x: 2, y: 2, z: 4, core: 2. Of those that a mesh axis runs over, the one named last changes fastest.
Arguments:
- block_input: float32 [4096, 2048], P(('dp', 'row'), 'col'), as said below
- out_grad: float32 [4096, 2048], P(('dp', 'row'), 'col'), may hold values from -6 to 6
- ln1_gain: float32 [2048], P('col'), may hold values from 0.25 to 1.75
- ln1_bias: float32 [2048], P('col'), may hold values from -1.75 to 1.75
- ln2_gain: float32 [2048], P('col'), may hold values from 0.25 to 1.75
- ln2_bias: float32 [2048], P('col'), may hold values from -1.75 to 1.75
- w_qkv: bfloat16 [2048, 6144], P('row', 'col'), as said below
- b_qkv: float32 [6144], P('col'), may hold values from -3 to 3
- w_dense: bfloat16 [2048, 2048], P('col', 'row'), may hold values from -0.5 to 0.5
- b_dense: float32 [2048], P('col'), may hold values from -1.75 to 1.75
- w_fc: bfloat16 [2048, 8192], P('row', 'col'), may hold values from -0.125 to 0.125
- b_fc: float32 [8192], P('col'), may hold values from -3 to 3
- w_proj: bfloat16 [8192, 2048], P('col', 'row'), may hold values from -0.0625 to 0.0625
- b_proj: float32 [2048], P('col'), may hold values from -1.75 to 1.75
Outputs:
- block_output: float32 [4096, 2048], P(('dp', 'row'), 'col')
- input_grad: float32 [4096, 2048], P(('dp', 'row'), 'col')
- grad_ln1_gain: float32 [2048], P('col')
- grad_ln1_bias: float32 [2048], P('col')
- grad_ln2_gain: float32 [2048], P('col')
- grad_ln2_bias: float32 [2048], P('col')
- grad_w_qkv: float32 [2048, 6144], P('row', 'col')
- grad_b_qkv: float32 [6144], P('col')
- grad_w_dense: float32 [2048, 2048], P('col', 'row')
- grad_b_dense: float32 [2048], P('col')
- grad_w_fc: float32 [2048, 8192], P('row', 'col')
- grad_b_fc: float32 [8192], P('col')
- grad_w_proj: float32 [8192, 2048], P('col', 'row')
- grad_b_proj: float32 [2048], P('col')
Inputs may be any that keep to these rules, and one draw needn't show every extreme that they name: `block_input`: finite real values. `w_qkv`: finite real values.
All inputs are finite; a program needn't handle non-finite values.
Results may differ from a plain program's by a relative error of at most 0.011.
Values may be sent and summed in bfloat16 or wider, within the bound.
A program may use at most 320 MiB of HBM per device.

v0:
```python
import math
import jax
import jax.numpy as jnp
from jax import lax
from jax.sharding import PartitionSpec as P

D = 2048
HD = 256
ROT = 64
SEQ = 512
epsilon = 1e-05
contract_last = (((1,), (1,)), ((), ()))
contract_first = (((0,), (0,)), ((), ()))


def angle_tables(length):
    half_rot = ROT // 2
    position = jnp.arange(length, dtype=jnp.float32)
    exponent = jnp.arange(half_rot, dtype=jnp.float32) * (2.0 / ROT)
    frequency = 10000.0 ** (-exponent)
    angles = position[:, None] * frequency[None, :]
    return (jnp.cos(angles), jnp.sin(angles))


def rotate_fwd(values, cosine, sine_vals):
    half_rot = ROT // 2
    first = values[..., :half_rot]
    second = values[..., half_rot:ROT]
    cos_part = cosine[:, None, :]
    sin_part = sine_vals[:, None, :]
    return jnp.concatenate(
        [
            first * cos_part - second * sin_part,
            second * cos_part + first * sin_part,
            values[..., ROT:],
        ],
        axis=-1,
    )


def rotate_back(grads, cosine, sine_vals):
    half_rot = ROT // 2
    first = grads[..., :half_rot]
    second = grads[..., half_rot:ROT]
    cos_part = cosine[:, None, :]
    sin_part = sine_vals[:, None, :]
    return jnp.concatenate(
        [
            first * cos_part + second * sin_part,
            second * cos_part - first * sin_part,
            grads[..., ROT:],
        ],
        axis=-1,
    )


def gelu_value(pre_act):
    return 0.5 * pre_act * (1.0 + lax.erf(pre_act * 0.7071067811865476))


def gelu_slope(pre_act):
    return 0.5 * (
        1.0 + lax.erf(pre_act * 0.7071067811865476)
    ) + pre_act * 0.3989422804014327 * jnp.exp(-0.5 * pre_act * pre_act)


def shards(
    block_input,
    out_grad,
    ln1_gain,
    ln1_bias,
    ln2_gain,
    ln2_bias,
    w_qkv,
    b_qkv,
    w_dense,
    b_dense,
    w_fc,
    b_fc,
    w_proj,
    b_proj,
):
    tok_rows = block_input.shape[0]
    seq_count = tok_rows // SEQ
    qkv_cols = w_qkv.shape[1]
    fc_cols = w_fc.shape[1]
    local_heads = qkv_cols // (3 * HD)
    head_cols = local_heads * HD
    scale = 1.0 / math.sqrt(HD)
    cosine, sine_vals = angle_tables(SEQ)
    causal = jnp.arange(SEQ)[:, None] >= jnp.arange(SEQ)[None, :]
    row_total, square_total = lax.psum(
        (jnp.sum(block_input, axis=1), jnp.sum(block_input * block_input, axis=1)), "col"
    )
    mean_row = (row_total / D)[:, None]
    var_row = (square_total / D)[:, None] - mean_row * mean_row
    inv_std = lax.rsqrt(var_row + epsilon)
    x_hat = (block_input - mean_row) * inv_std
    normed_one = (x_hat * ln1_gain + ln1_bias).astype(jnp.bfloat16)
    normed_two = (x_hat * ln2_gain + ln2_bias).astype(jnp.bfloat16)
    wide_one, wide_two = (
        lax.all_gather(normed_one, "col", axis=1, tiled=True),
        lax.all_gather(normed_two, "col", axis=1, tiled=True),
    )
    part_one = wide_one
    part_two = wide_two
    qkv_pre = jnp.dot(
        part_one,
        lax.all_gather(w_qkv, "row", axis=0, tiled=True),
        preferred_element_type=jnp.float32,
    )
    fc_pre = jnp.dot(
        part_two,
        lax.all_gather(w_fc, "row", axis=0, tiled=True),
        preferred_element_type=jnp.float32,
    )
    qkv_pre = qkv_pre + b_qkv
    fc_pre = fc_pre + b_fc

    def forward_seq(block):
        query = rotate_fwd(block[:, :, 0], cosine, sine_vals).astype(jnp.bfloat16)
        keys = rotate_fwd(block[:, :, 1], cosine, sine_vals).astype(jnp.bfloat16)
        values = block[:, :, 2].astype(jnp.bfloat16)
        scores = jnp.einsum("qhd,khd->hqk", query, keys, preferred_element_type=jnp.float32) * scale
        masked = jnp.where(causal[None], scores, -1e30)
        row_max = jnp.max(masked, axis=-1, keepdims=True)
        exp_sum = jnp.sum(
            jnp.where(causal[None], jnp.exp(masked - row_max), 0.0), axis=-1, keepdims=True
        )
        log_total = row_max + jnp.log(exp_sum)
        probs_low = jnp.where(causal[None], jnp.exp(masked - log_total), 0.0).astype(jnp.bfloat16)
        attended = jnp.einsum(
            "hqk,khd->qhd", probs_low, values, preferred_element_type=jnp.float32
        ).astype(jnp.bfloat16)
        return (query, keys, values, attended, log_total)

    query, keys, values, attended, log_total = lax.map(
        forward_seq, qkv_pre.reshape(seq_count, SEQ, local_heads, 3, HD)
    )
    attn_out = attended.reshape(tok_rows, head_cols)
    gelu_out = gelu_value(fc_pre).astype(jnp.bfloat16)
    out_stack = jnp.concatenate([w_dense, w_proj], axis=0)
    shard_piece = lax.all_gather(out_stack, "row", axis=1, tiled=True)
    mixed = jnp.dot(
        attn_out, shard_piece[:head_cols], preferred_element_type=jnp.float32
    ) + jnp.dot(gelu_out, shard_piece[head_cols:], preferred_element_type=jnp.float32)
    branch_sum = lax.psum_scatter(mixed, "col", scatter_dimension=1, tiled=True)
    block_output = block_input + branch_sum + b_dense + b_proj
    grad_low = out_grad.astype(jnp.bfloat16)
    wide_grad = lax.all_gather(grad_low, "col", axis=1, tiled=True)
    both_grad = lax.dot_general(
        wide_grad,
        lax.all_gather(out_stack, "row", axis=1, tiled=True),
        contract_last,
        preferred_element_type=jnp.float32,
    )
    attn_grad = both_grad[:, :head_cols]
    gelu_grad = both_grad[:, head_cols:]
    attn_grad_low = attn_grad.astype(jnp.bfloat16)
    fc_grad = gelu_grad * gelu_slope(fc_pre)
    fc_bias_grad = jnp.sum(fc_grad, axis=0)
    fc_grad_low = fc_grad.astype(jnp.bfloat16)

    def backward_seq(items):
        query_s, keys_s, values_s, attended_s, log_s, head_grad = items
        scores = (
            jnp.einsum("qhd,khd->hqk", query_s, keys_s, preferred_element_type=jnp.float32) * scale
        )
        probs = jnp.where(
            causal[None], jnp.exp(jnp.where(causal[None], scores, -1e30) - log_s), 0.0
        )
        probs_low = probs.astype(jnp.bfloat16)
        value_grad = jnp.einsum(
            "hqk,qhd->khd", probs_low, head_grad, preferred_element_type=jnp.float32
        )
        prob_grad = jnp.einsum(
            "qhd,khd->hqk", head_grad, values_s, preferred_element_type=jnp.float32
        )
        delta_row = jnp.transpose(
            jnp.sum(head_grad.astype(jnp.float32) * attended_s.astype(jnp.float32), axis=-1), (1, 0)
        )[:, :, None]
        score_grad = (probs * (prob_grad - delta_row) * scale).astype(jnp.bfloat16)
        query_grad = jnp.einsum(
            "hqk,khd->qhd", score_grad, keys_s, preferred_element_type=jnp.float32
        )
        key_grad = jnp.einsum(
            "hqk,qhd->khd", score_grad, query_s, preferred_element_type=jnp.float32
        )
        return jnp.stack(
            [
                rotate_back(query_grad, cosine, sine_vals),
                rotate_back(key_grad, cosine, sine_vals),
                value_grad,
            ],
            axis=2,
        )

    head_grads = attn_grad_low.reshape(seq_count, SEQ, local_heads, HD)
    qkv_grad = lax.map(
        backward_seq, (query, keys, values, attended, log_total, head_grads)
    ).reshape(tok_rows, qkv_cols)
    qkv_bias_grad = jnp.sum(qkv_grad, axis=0)
    qkv_grad_low = qkv_grad.astype(jnp.bfloat16)
    in_stack = jnp.concatenate([w_qkv, w_fc], axis=1)
    shard_piece = lax.all_gather(in_stack, "row", axis=0, tiled=True)
    norm_grads = jnp.stack(
        [
            lax.dot_general(
                qkv_grad_low,
                shard_piece[:, :qkv_cols],
                contract_last,
                preferred_element_type=jnp.float32,
            ),
            lax.dot_general(
                fc_grad_low,
                shard_piece[:, qkv_cols:],
                contract_last,
                preferred_element_type=jnp.float32,
            ),
        ]
    )
    part_one = wide_one
    part_two = wide_two
    row_part = lax.psum_scatter(
        jnp.concatenate(
            [
                lax.dot_general(
                    part_one, qkv_grad_low, contract_first, preferred_element_type=jnp.float32
                ),
                lax.dot_general(
                    part_two, fc_grad_low, contract_first, preferred_element_type=jnp.float32
                ),
                lax.dot_general(
                    wide_grad, attn_out, contract_first, preferred_element_type=jnp.float32
                ),
                lax.dot_general(
                    wide_grad, gelu_out, contract_first, preferred_element_type=jnp.float32
                ),
            ],
            axis=1,
        ),
        "row",
        scatter_dimension=0,
        tiled=True,
    )
    grad_rows = lax.psum(row_part, "dp")
    qkv_total = grad_rows[:, :qkv_cols]
    fc_total = grad_rows[:, qkv_cols : qkv_cols + fc_cols]
    dense_total = grad_rows[:, qkv_cols + fc_cols : qkv_cols + fc_cols + head_cols].T
    proj_total = grad_rows[:, qkv_cols + fc_cols + head_cols :].T
    norm_local = lax.psum_scatter(norm_grads, "col", scatter_dimension=2, tiled=True)
    grad_one = norm_local[0]
    grad_two = norm_local[1]
    hat_grad = grad_one * ln1_gain + grad_two * ln2_gain
    total_hat, total_cross = lax.psum(
        (jnp.sum(hat_grad, axis=1), jnp.sum(hat_grad * x_hat, axis=1)), "col"
    )
    input_grad = out_grad + inv_std * (
        hat_grad - (total_hat / D)[:, None] - x_hat * (total_cross / D)[:, None]
    )
    gain_one, shift_one, gain_two, shift_two, qkv_bias_total, fc_bias_total, out_bias_total = (
        lax.psum(
            (
                jnp.sum(grad_one * x_hat, axis=0),
                jnp.sum(grad_one, axis=0),
                jnp.sum(grad_two * x_hat, axis=0),
                jnp.sum(grad_two, axis=0),
                qkv_bias_grad,
                fc_bias_grad,
                jnp.sum(out_grad, axis=0),
            ),
            ("dp", "row"),
        )
    )
    return (
        block_output,
        input_grad,
        gain_one,
        shift_one,
        gain_two,
        shift_two,
        qkv_total,
        qkv_bias_total,
        dense_total,
        out_bias_total,
        fc_total,
        fc_bias_total,
        proj_total,
        out_bias_total,
    )


def solution(mesh):
    return jax.shard_map(
        shards,
        mesh=mesh,
        in_specs=(
            P(("dp", "row"), "col"),
            P(("dp", "row"), "col"),
            P("col"),
            P("col"),
            P("col"),
            P("col"),
            P("row", "col"),
            P("col"),
            P("col", "row"),
            P("col"),
            P("row", "col"),
            P("col"),
            P("col", "row"),
            P("col"),
        ),
        out_specs=(
            P(("dp", "row"), "col"),
            P(("dp", "row"), "col"),
            P("col"),
            P("col"),
            P("col"),
            P("col"),
            P("row", "col"),
            P("col"),
            P("col", "row"),
            P("col"),
            P("row", "col"),
            P("col"),
            P("col", "row"),
            P("col"),
        ),
        check_vma=False,
    )
```

profile of v0, /device:TPU:0, one launch (start us, length us, event | category | flops | bytes accessed | tf_op | source)
XLA Modules:
  0.0 1304.8 jit_solution(7486907103567437499)
XLA Ops:
  8.9 13.5 %all-reduce.2 = (f32[512]{0:T(512)S(1)}, f32[512]{0:T(512)S(1)}) all-reduce(f32[512]{0:T(512)S(1)} %get-tuple-element.126, f32[512]{0:T(512)S(1)} %get-tuple-element.125), channel_id=1, replica_groups=mesh['dp'=2,'row'=4,'col'=4] {'col'}, use_global_device_ids=true, to_apply=%region_3.0 | all-reduce | flops 1024 | bytes 8192 | tf_op jit(solution)/shard_map/psum | solution.py:92
  22.4 2.6 add_convert_fusion.1
  27.3 3.4 pad_maximum_fusion.4
  32.0 3.6 pad_maximum_fusion.2
  36.4 1.7 fusion.28
  38.1 30.9 %all-gather.8.cloned.1.call-done = bf16[512,2048]{1,0:T(8,128)(2,1)} async-done(((bf16[512,512]{1,0:T(8,128)(2,1)}), bf16[512,2048]{1,0:T(8,128)(2,1)}) %all-gather.8.cloned.1.call-update) | async-done | bytes 2097168 | tf_op jit(solution)/shard_map/all_gather | solution.py:102
  69.0 70.7 %all-gather.10.cloned.1.call-done = bf16[2048,1536]{1,0:T(8,128)(2,1)} async-done(((bf16[512,1536]{1,0:T(8,128)(2,1)}), bf16[2048,1536]{1,0:T(8,128)(2,1)}) %all-gather.10.cloned.1.call-update) | async-done | bytes 6291472 | tf_op jit(solution)/shard_map/all_gather | solution.py:109
  139.7 8.5 convolution_add_fusion.1
  148.2 2.6 copy.68
  152.3 2.5 copy.104
  154.8 2.3 slice.195
  157.0 2.5 copy.103
  161.1 2.3 subtract_convert_fusion.1
  166.4 21.1 %all-gather.18.cloned.1.call-done = bf16[512,2048]{1,0:T(8,128)(2,1)} async-done(((bf16[512,512]{1,0:T(8,128)(2,1)}), bf16[512,2048]{1,0:T(8,128)(2,1)}) %all-gather.18.cloned.1.call-update) | async-done | bytes 2097168 | tf_op jit(solution)/shard_map/all_gather | solution.py:150
  187.5 105.9 %all-gather.12.cloned.1.call-done = bf16[2560,2048]{1,0:T(8,128)(2,1)} async-done(((bf16[2560,512]{1,0:T(8,128)(2,1)}), bf16[2560,2048]{1,0:T(8,128)(2,1)}) %all-gather.12.cloned.1.call-update) | async-done | bytes 10485776 | tf_op jit(solution)/shard_map/all_gather | solution.py:143
  293.4 9.5 convolution_bitcast_fusion.1
  302.9 2.4 copy-done.28
  306.2 2.0 copy.74
  308.3 3.4 multiply_reduce_fusion.1
  319.1 2.6 copy.86
  321.8 5.0 convolution_bitcast_fusion.2
  326.8 6.3 fusion.42
  333.1 7.4 all-gather.14.cloned.1.call-done
  340.5 88.0 %all-gather.16.cloned.1.call-done = bf16[2048,2048]{1,0:T(8,128)(2,1)} async-done(((bf16[512,2048]{1,0:T(8,128)(2,1)}), bf16[2048,2048]{1,0:T(8,128)(2,1)}) %all-gather.16.cloned.1.call-update) | async-done | bytes 8388624 | tf_op jit(solution)/shard_map/all_gather | solution.py:114
  428.6 9.9 fusion.36
  438.5 9.2 fusion.23
  448.2 8.3 convolution_bitcast_fusion
  456.5 32.9 %pad_maximum_fusion = f32[2048,6144]{0,1:T(8,128)} fusion(f32[2048,2048]{0,1:T(8,128)} %convolution_bitcast_fusion, f32[2048,512]{0,1:T(8,128)S(1)} %copy-done, f32[2048,2048]{0,1:T(8,128)} %fusion.23, f32[2048,1536]{0,1:T(8,128)} %fusion.42), kind=kLoop, calls=%fused_computation | loop fusion | flops 37748736 | bytes 100663296 | tf_op jit(solution)/shard_map/concatenate | solution.py:225
  489.4 80.8 %all-gather.20.cloned.1.call-done = bf16[2048,3584]{1,0:T(8,128)(2,1)} async-done(((bf16[512,3584]{1,0:T(8,128)(2,1)}), bf16[2048,3584]{1,0:T(8,128)(2,1)}) %all-gather.20.cloned.1.call-update) | async-done | bytes 14680080 | tf_op jit(solution)/shard_map/all_gather | solution.py:205
  570.3 6.2 fusion.10
  576.5 7.0 fusion.13
  583.5 3.8 pad_maximum_fusion.1
  587.6 9.5 fusion.2
  597.0 5.0 convolution_add_fusion
  602.1 395.2 %reduce-scatter.8.cloned.1.call-done = f32[512,6144]{0,1:T(8,128)} async-done(((f32[2048,6144]{0,1:T(8,128)}), f32[512,6144]{0,1:T(8,128)}) %reduce-scatter.8.cloned.1.call-update) | async-done | bytes 12582928 | tf_op jit(solution)/shard_map/reduce_scatter | solution.py:224
  999.0 145.4 %reduce-scatter.6.cloned.1.call-done = f32[2,512,512]{2,1,0:T(8,128)} async-done(((f32[2,512,2048]{2,1,0:T(8,128)}), f32[2,512,512]{2,1,0:T(8,128)}) %reduce-scatter.6.cloned.1.call-update) | async-done | bytes 2097168 | tf_op jit(solution)/shard_map/reduce_scatter | solution.py:251
  1144.3 1.7 slice_reduce_fusion
  1146.1 2.2 fusion.21
  1148.3 27.5 %all-reduce = (f32[512]{0:T(512)}, f32[512]{0:T(512)}, f32[512]{0:T(512)}, f32[512]{0:T(512)}, f32[1536]{0:T(1024)}, /*index=5*/f32[512]{0:T(512)S(1)}, f32[2048]{0:T(1024)}) all-reduce(f32[512]{0:T(512)S(1)} %get-tuple-element.120, f32[512]{0:T(512)S(1)} %get-tuple-element.122, ...), channel_id=1, replica_groups=mesh['dp'=2,'row'=4,'col'=4] {'dp','row'}, use_global_device_ids=true, to_apply=%region_14.15 | all-reduce | flops 6144 | bytes 49152 | tf_op jit(solution)/shard_map/psum | solution.py:262
  1175.8 12.4 all-reduce.1
  1188.2 36.5 %reduce-scatter.4.cloned.1.call-done = f32[512,512]{1,0:T(8,128)} async-done(((f32[512,2048]{1,0:T(8,128)}), f32[512,512]{1,0:T(8,128)}) %reduce-scatter.4.cloned.1.call-update) | async-done | bytes 1048592 | tf_op jit(solution)/shard_map/reduce_scatter | solution.py:147
  1224.8 2.9 multiply_add_fusion
  1227.7 50.2 %all-reduce.5.cloned.1.call-done = f32[512,6144]{0,1:T(8,128)} async-done(((f32[512,6144]{0,1:T(8,128)}), f32[512,6144]{0,1:T(8,128)}) %all-reduce.5.cloned.1.call-update) | async-done | bytes 12582928 | tf_op jit(solution)/shard_map/psum | solution.py:246
  1277.9 1.9 slice-done
  1279.7 2.4 copy.88
  1282.1 7.7 slice_bitcast_fusion
  1289.8 5.3 copy.89
  1295.2 2.3 slice_bitcast_fusion.1
  (140 shorter events, 23.3 us)
Async XLA Ops:
  7.2 18.6 %copy-start.6 = (f32[512,512]{1,0:T(8,128)S(1)}, f32[512,512]{1,0:T(8,128)}, u32[]{:S(2)}) copy-start(f32[512,512]{1,0:T(8,128)} %param.15) | copy-start | bytes 3145732
  7.2 20.1 %copy-start.27 = (bf16[512,512]{1,0:T(8,128)(2,1)S(1)}, bf16[512,512]{1,0:T(8,128)(2,1)}, u32[]{:S(2)}) copy-start(bf16[512,512]{1,0:T(8,128)(2,1)} %param.22) | copy-start | bytes 1572868
  7.2 61.8 %all-gather.8.cloned.1.call-start = ((), (), s32[]{:S(2)}) async-start(), calls=%async_computation.3 | async-start | bytes 2621440 | tf_op jit(solution)/shard_map/all_gather | solution.py:102
  22.4 4.9 copy-start.29
  22.4 4.9 copy-start.31
  25.0 114.7 %all-gather.10.cloned.1.call-start = ((), (), s32[]{:S(2)}) async-start(), calls=%async_computation.4 | async-start | bytes 7864320 | tf_op jit(solution)/shard_map/all_gather | solution.py:109
  25.7 161.8 %all-gather.18.cloned.1.call-start = ((), (), s32[]{:S(2)}) async-start(), calls=%async_computation.9 | async-start | bytes 2621440 | tf_op jit(solution)/shard_map/all_gather | solution.py:150
  27.2 4.7 copy-start.3
  27.3 266.2 %all-gather.12.cloned.1.call-start = ((), (), s32[]{:S(2)}) async-start(), calls=%async_computation.5 | async-start | bytes 13107200 | tf_op jit(solution)/shard_map/all_gather | solution.py:143
  30.7 309.8 %all-gather.14.cloned.1.call-start = ((), (), s32[]{:S(2)}) async-start(), calls=%async_computation.6 | async-start | bytes 2621440 | tf_op jit(solution)/shard_map/all_gather | solution.py:103
  31.3 397.2 %all-gather.16.cloned.1.call-start = ((), (), s32[]{:S(2)}) async-start(), calls=%async_computation.7 | async-start | bytes 10485760 | tf_op jit(solution)/shard_map/all_gather | solution.py:114
  31.9 107.8 %copy-start.41 = (f32[1536]{0:T(1024)S(1)}, f32[1536]{0:T(1024)}, u32[]{:S(2)}) copy-start(f32[1536]{0:T(1024)} %param.21) | copy-start | bytes 18436
  31.9 538.3 %all-gather.20.cloned.1.call-start = ((), (), s32[]{:S(2)}) async-start(), calls=%async_computation.10 | async-start | bytes 18350080 | tf_op jit(solution)/shard_map/all_gather | solution.py:205
  35.6 961.8 %reduce-scatter.8.cloned.1.call-start = ((), (), s32[]{:S(2)}) async-start(), calls=%async_computation.12 | async-start | bytes 62914560 | tf_op jit(solution)/shard_map/reduce_scatter | solution.py:224
  159.6 3.9 copy-start.10
  159.6 3.9 copy-start.16
  161.1 3.5 copy-start.14
  163.4 3.0 copy-start.19
  163.4 3.0 copy-start.21
  308.2 3.5 copy-start.5
  308.2 3.5 copy-start.11
  308.2 3.5 copy-start.12
  308.2 4.4 copy-start.17
  308.2 4.4 copy-start.24
  308.2 4.4 copy-start.26
  317.1 4.6 copy-start.8
  321.7 5.0 copy-start.18
  321.7 5.0 copy-start.39
  326.8 101.8 %copy-start.42 = (f32[2048]{0:T(1024)S(1)}, f32[2048]{0:T(1024)}, u32[]{:S(2)}) copy-start(f32[2048]{0:T(1024)} %param.25) | copy-start | bytes 24580
  428.6 9.9 copy-start.40
  438.5 9.2 copy-start.43
  438.5 9.7 copy-start.45
  438.5 9.7 copy-start.13
  448.2 8.3 copy-start
  489.4 655.0 %reduce-scatter.6.cloned.1.call-start = ((), (), s32[]{:S(2)}) async-start(), calls=%async_computation.11 | async-start | bytes 10485760 | tf_op jit(solution)/shard_map/reduce_scatter | solution.py:251
  570.3 6.2 copy-start.44
  587.3 637.4 %reduce-scatter.4.cloned.1.call-start = ((), (), s32[]{:S(2)}) async-start(), calls=%async_computation.8 | async-start | bytes 5242880 | tf_op jit(solution)/shard_map/reduce_scatter | solution.py:147
  602.0 675.8 %all-reduce.5.cloned.1.call-start = ((), (), s32[]{:S(2)}) async-start(), calls=%async_computation.13 | async-start | bytes 25165824 | tf_op jit(solution)/shard_map/psum | solution.py:246
  997.4 148.7 %copy-start.1 = (f32[512,512]{1,0:T(8,128)S(1)}, f32[512,512]{1,0:T(8,128)}, u32[]{:S(2)}) copy-start(f32[512,512]{1,0:T(8,128)} %param.14) | copy-start | bytes 3145732
  997.4 148.7 %copy-start.30 = (f32[512]{0:T(512)S(1)}, f32[512]{0:T(512)}, u32[]{:S(2)}) copy-start(f32[512]{0:T(512)} %copy-done.29) | copy-start | bytes 6148
  997.4 148.7 %copy-start.32 = (f32[512]{0:T(512)S(1)}, f32[512]{0:T(512)}, u32[]{:S(2)}) copy-start(f32[512]{0:T(512)} %copy-done.31) | copy-start | bytes 6148
  997.4 148.7 %copy-start.34 = (f32[512]{0:T(512)S(1)}, f32[512]{0:T(512)}, u32[]{:S(2)}) copy-start(f32[512]{0:T(512)} %param.16) | copy-start | bytes 6148
  997.4 148.7 %copy-start.35 = (f32[512]{0:T(512)S(1)}, f32[512]{0:T(512)}, u32[]{:S(2)}) copy-start(f32[512]{0:T(512)} %param.18) | copy-start | bytes 6148
  997.4 150.9 %copy-start.33 = (f32[512]{0:T(512)S(1)}, f32[512]{0:T(512)}, u32[]{:S(2)}) copy-start(f32[512]{0:T(512)} %get-tuple-element.155) | copy-start | bytes 6148
  997.4 227.3 %copy-start.36 = (f32[512]{0:T(512)S(1)}, f32[512]{0:T(512)}, u32[]{:S(2)}) copy-start(f32[512]{0:T(512)} %param.27) | copy-start | bytes 6148
  997.4 227.3 %copy-start.37 = (f32[512]{0:T(512)S(1)}, f32[512]{0:T(512)}, u32[]{:S(2)}) copy-start(f32[512]{0:T(512)} %param.23) | copy-start | bytes 6148
  998.9 225.8 %copy-start.7 = (f32[512,512]{1,0:T(8,128)S(1)}, f32[512,512]{1,0:T(8,128)}, u32[]{:S(2)}) copy-start(f32[512,512]{1,0:T(8,128)} %param.15) | copy-start | bytes 3145732
  1175.8 121.7 %copy-start.38 = (f32[512]{0:T(512)}, f32[512]{0:T(512)S(1)}, u32[]{:S(2)}) copy-start(f32[512]{0:T(512)S(1)} %get-tuple-element.204) | copy-start | bytes 6148
  (10 other events, 20.6 us)
Sparse Core Ops, SparseCore 0:
  25.1 43.8 all-gather.7
  70.8 68.8 all-gather.9
  141.8 45.6 all-gather.17
  189.8 103.5 all-gather.11
  294.8 45.6 all-gather.13
  342.2 86.2 all-gather.15
  430.4 139.8 all-gather.19
  573.4 423.9 reduce-scatter.7
  999.7 144.6 reduce-scatter.5
  1147.1 77.6 reduce-scatter.3
  1227.3 50.5 all-reduce.4
where the time goes:
time: 1310 us; the launch traced here: 1300 us
  waiting for transfers between devices  1030 us (79%)
  matrix products  91.9 us (7%)
  other arithmetic  65.9 us (5%)
  blocking collectives  53.4 us (4%)
  local copies, waits for them, and re-layouts  44.1 us (3%)
  between operations  14.7 us (1%)
    reduce_scatter x1, waiting for transfers between devices, shards(): lax.psum_scatter(jnp.concatenate([lax.dot_general(part_one, qkv_grad_low,...  395 us
    reduce_scatter x1, waiting for transfers between devices, shards(): lax.psum_scatter(norm_grads, 'col', scatter_dimension=2, tiled=True)  145 us
    all_gather x1, waiting for transfers between devices, shards(): shard_piece = lax.all_gather(out_stack, 'row', axis=1, tiled=True)  106 us
    all_gather x1, waiting for transfers between devices, shards(): lax.all_gather(w_fc, 'row', axis=0, tiled=True)  88 us
    all_gather x1, waiting for transfers between devices, shards(): shard_piece = lax.all_gather(in_stack, 'row', axis=0, tiled=True)  80.8 us
    all_gather x1, waiting for transfers between devices, shards(): lax.all_gather(w_qkv, 'row', axis=0, tiled=True)  70.7 us
    psum x1, waiting for transfers between devices, shards(): grad_rows = lax.psum(row_part, 'dp')  50.2 us
    reduce_scatter x1, waiting for transfers between devices, shards(): branch_sum = lax.psum_scatter(mixed, 'col', scatter_dimension=1, tiled=True)  36.5 us
  transfers between devices with their start and end apart: 11, of which 11 were waited for; matrix products, arithmetic and copies ran while one was open for 13% of the time, Pallas kernels for 0%

commit v1 on v0

--- a/solution.py
+++ b/solution.py
@@ -11,6 +11,18 @@
 epsilon = 1e-05
 contract_last = (((1,), (1,)), ((), ()))
 contract_first = (((0,), (0,)), ((), ()))
+
+
+def collect(value, axis, dim):
+    ways, here = (lax.axis_size(axis), lax.axis_index(axis))
+    grown, reach = (value, 1)
+    while reach < ways:
+        theirs = lax.ppermute(grown, axis, [(d, d ^ reach) for d in range(ways)])
+        mine_first = jnp.concatenate([grown, theirs], axis=dim)
+        theirs_first = jnp.concatenate([theirs, grown], axis=dim)
+        grown = jnp.where(here & reach == 0, mine_first, theirs_first)
+        reach = 2 * reach
+    return grown
 
 
 def angle_tables(length):
@@ -109,11 +121,7 @@
         lax.all_gather(w_qkv, "row", axis=0, tiled=True),
         preferred_element_type=jnp.float32,
     )
-    fc_pre = jnp.dot(
-        part_two,
-        lax.all_gather(w_fc, "row", axis=0, tiled=True),
-        preferred_element_type=jnp.float32,
-    )
+    fc_pre = jnp.dot(part_two, collect(w_fc, "row", 0), preferred_element_type=jnp.float32)
     qkv_pre = qkv_pre + b_qkv
     fc_pre = fc_pre + b_fc
 

time: 1310 us -> 1270 us (0.969)
  waiting for transfers between devices: 1030 us -> 982 us
    all_gather x1 -> x0, waiting for transfers between devices: 88 us -> none  [shards(): lax.all_gather(w_fc, 'row', axis=0, tiled=True)]
    ppermute x0 -> x2, waiting for transfers between devices: none -> 42.1 us  [collect(): theirs = lax.ppermute(grown, axis, [(d, d ^ reach) for d in range(ways)])]
    all_gather x1, waiting for transfers between devices: 30.9 us -> 0.01 us  [shards(): lax.all_gather(normed_one, 'col', axis=1, tiled=True)]
    all_gather x1, waiting for transfers between devices: 70.7 us -> 101 us  [shards(): lax.all_gather(w_qkv, 'row', axis=0, tiled=True)]
  transfers between devices with their start and end apart: 11 -> 12, of which waited for: 11 -> 10; matrix products, arithmetic and copies ran while one was open for 13% -> 14% of each run, Pallas kernels for 0% -> 0%
where the time goes in v1:
time: 1270 us; the launch traced here: 1260 us
  waiting for transfers between devices  982 us (77%)
  matrix products  94.5 us (7%)
  other arithmetic  72.6 us (6%)
  blocking collectives  53.3 us (4%)
  local copies, waits for them, and re-layouts  43.5 us (3%)
  between operations  15 us (1%)
    reduce_scatter x1, waiting for transfers between devices, shards(): lax.psum_scatter(jnp.concatenate([lax.dot_general(part_one, qkv_grad_low,...  395 us
    reduce_scatter x1, waiting for transfers between devices, shards(): lax.psum_scatter(norm_grads, 'col', scatter_dimension=2, tiled=True)  145 us
    all_gather x1, waiting for transfers between devices, shards(): shard_piece = lax.all_gather(out_stack, 'row', axis=1, tiled=True)  106 us
    all_gather x1, waiting for transfers between devices, shards(): lax.all_gather(w_qkv, 'row', axis=0, tiled=True)  101 us
    all_gather x1, waiting for transfers between devices, shards(): shard_piece = lax.all_gather(in_stack, 'row', axis=0, tiled=True)  76.3 us
    psum x1, waiting for transfers between devices, shards(): grad_rows = lax.psum(row_part, 'dp')  50 us
    ppermute x2, waiting for transfers between devices, collect(): theirs = lax.ppermute(grown, axis, [(d, d ^ reach) for d in range(ways)])  42.1 us
    reduce_scatter x1, waiting for transfers between devices, shards(): branch_sum = lax.psum_scatter(mixed, 'col', scatter_dimension=1, tiled=True)  36.8 us
  transfers between devices with their start and end apart: 12, of which 10 were waited for; matrix products, arithmetic and copies ran while one was open for 14% of the time, Pallas kernels for 0%

profile of v1, /device:TPU:0, one launch (start us, length us, event | category | flops | bytes accessed | tf_op | source)
XLA Modules:
  0.0 1263.7 jit_solution(15780885147799556896)
XLA Ops:
  8.9 13.5 %all-reduce.2 = (f32[512]{0:T(512)S(1)}, f32[512]{0:T(512)S(1)}) all-reduce(f32[512]{0:T(512)S(1)} %get-tuple-element.126, f32[512]{0:T(512)S(1)} %get-tuple-element.125), channel_id=1, replica_groups=mesh['dp'=2,'row'=4,'col'=4] {'col'}, use_global_device_ids=true, to_apply=%region_3.0 | all-reduce | flops 1024 | bytes 8192 | tf_op jit(solution)/shard_map/psum | solution.py:104
  22.4 2.6 add_convert_fusion.1
  27.3 3.4 pad_maximum_fusion.4
  31.4 3.7 pad_maximum_fusion.2
  37.5 1.7 fusion.35
  39.2 42.1 %collective-permute-done = bf16[512,2048]{1,0:T(8,128)(2,1)} collective-permute-done((bf16[512,2048]{1,0:T(8,128)(2,1)S(1)}, bf16[512,2048]{1,0:T(8,128)(2,1)}, u32[]{:S(2)}, u32[]{:S(2)}) %collective-permute-start) | collective-permute-done | bytes 2097184 | tf_op jit(solution)/shard_map/ppermute | solution.py:20
  81.2 5.2 maximum_select_fusion.2
  87.5 100.8 %all-gather.9.cloned.1.call-done = bf16[2048,1536]{1,0:T(8,128)(2,1)} async-done(((bf16[512,1536]{1,0:T(8,128)(2,1)}), bf16[2048,1536]{1,0:T(8,128)(2,1)}) %all-gather.9.cloned.1.call-update) | async-done | bytes 6291472 | tf_op jit(solution)/shard_map/all_gather | solution.py:121
  188.3 8.5 convolution_add_fusion.1
  196.8 2.5 copy.68
  200.8 2.5 copy.104
  203.3 2.3 slice.195
  205.6 2.5 copy.103
  209.7 2.3 subtract_convert_fusion.1
  215.0 20.5 %all-gather.15.cloned.1.call-done = bf16[512,2048]{1,0:T(8,128)(2,1)} async-done(((bf16[512,512]{1,0:T(8,128)(2,1)}), bf16[512,2048]{1,0:T(8,128)(2,1)}) %all-gather.15.cloned.1.call-update) | async-done | bytes 2097168 | tf_op jit(solution)/shard_map/all_gather | solution.py:158
  235.5 105.9 %all-gather.11.cloned.1.call-done = bf16[2560,2048]{1,0:T(8,128)(2,1)} async-done(((bf16[2560,512]{1,0:T(8,128)(2,1)}), bf16[2560,2048]{1,0:T(8,128)(2,1)}) %all-gather.11.cloned.1.call-update) | async-done | bytes 10485776 | tf_op jit(solution)/shard_map/all_gather | solution.py:151
  341.4 9.5 convolution_bitcast_fusion.1
  350.9 2.3 copy-done.28
  354.1 2.0 copy.74
  356.2 3.4 multiply_reduce_fusion.1
  367.0 2.6 copy.86
  369.7 5.1 convolution_bitcast_fusion.2
  374.8 6.4 fusion.50
  381.2 7.3 all-gather.13.cloned.1.call-done
  388.5 12.9 %fusion.44 = (f32[2048]{0:T(1024)S(1)}, bf16[512,2048]{1,0:T(8,128)(2,1)S(1)}, f32[512,2048]{1,0:T(8,128)}) fusion(f32[2048]{0:T(1024)S(1)} %copy-done.42, f32[512,2560]{1,0:T(8,128)} %copy-done.28, bf16[512,2048]{1,0:T(8,128)(2,1)} %all-gather.13.cloned.1.call-done, bf16[1024,2048]{1,0:T(8,128)(2,1)} %collective-permute-done.1, ...), kind=kOutput, calls=%fused_computation.99 | convolution fusion | flops 4345296896 | bytes 20987904 | tf_op jit(solution)/shard_map/dot_general | solution.py:124
  401.5 8.6 fusion.30
  410.1 8.3 convolution_bitcast_fusion
  418.4 34.2 %pad_maximum_fusion = f32[2048,6144]{0,1:T(8,128)} fusion(f32[2048,2048]{0,1:T(8,128)} %convolution_bitcast_fusion, f32[2048,512]{0,1:T(8,128)S(1)} %copy-done, f32[2048,2048]{0,1:T(8,128)} %fusion.30, f32[2048,1536]{0,1:T(8,128)} %fusion.50), kind=kLoop, calls=%fused_computation | loop fusion | flops 37748736 | bytes 100663296 | tf_op jit(solution)/shard_map/concatenate | solution.py:233
  452.6 76.3 %all-gather.17.cloned.1.call-done = bf16[2048,3584]{1,0:T(8,128)(2,1)} async-done(((bf16[512,3584]{1,0:T(8,128)(2,1)}), bf16[2048,3584]{1,0:T(8,128)(2,1)}) %all-gather.17.cloned.1.call-update) | async-done | bytes 14680080 | tf_op jit(solution)/shard_map/all_gather | solution.py:213
  528.9 6.2 fusion.17
  535.2 7.0 fusion.20
  542.1 3.8 pad_maximum_fusion.1
  546.2 9.5 fusion.2
  555.7 5.0 convolution_add_fusion
  560.7 395.2 %reduce-scatter.8.cloned.1.call-done = f32[512,6144]{0,1:T(8,128)} async-done(((f32[2048,6144]{0,1:T(8,128)}), f32[512,6144]{0,1:T(8,128)}) %reduce-scatter.8.cloned.1.call-update) | async-done | bytes 12582928 | tf_op jit(solution)/shard_map/reduce_scatter | solution.py:232
  957.6 145.4 %reduce-scatter.6.cloned.1.call-done = f32[2,512,512]{2,1,0:T(8,128)} async-done(((f32[2,512,2048]{2,1,0:T(8,128)}), f32[2,512,512]{2,1,0:T(8,128)}) %reduce-scatter.6.cloned.1.call-update) | async-done | bytes 2097168 | tf_op jit(solution)/shard_map/reduce_scatter | solution.py:259
  1103.0 1.7 slice_reduce_fusion
  1104.7 2.2 fusion.28
  1107.0 27.5 %all-reduce = (f32[512]{0:T(512)}, f32[512]{0:T(512)}, f32[512]{0:T(512)}, f32[512]{0:T(512)}, f32[1536]{0:T(1024)}, /*index=5*/f32[512]{0:T(512)S(1)}, f32[2048]{0:T(1024)}) all-reduce(f32[512]{0:T(512)S(1)} %get-tuple-element.120, f32[512]{0:T(512)S(1)} %get-tuple-element.122, ...), channel_id=1, replica_groups=mesh['dp'=2,'row'=4,'col'=4] {'dp','row'}, use_global_device_ids=true, to_apply=%region_14.15 | all-reduce | flops 6144 | bytes 49152 | tf_op jit(solution)/shard_map/psum | solution.py:270
  1134.4 12.4 all-reduce.1
  1146.8 36.8 %reduce-scatter.4.cloned.1.call-done = f32[512,512]{1,0:T(8,128)} async-done(((f32[512,2048]{1,0:T(8,128)}), f32[512,512]{1,0:T(8,128)}) %reduce-scatter.4.cloned.1.call-update) | async-done | bytes 1048592 | tf_op jit(solution)/shard_map/reduce_scatter | solution.py:155
  1183.6 2.9 multiply_add_fusion
  1186.5 50.0 %all-reduce.5.cloned.1.call-done = f32[512,6144]{0,1:T(8,128)} async-done(((f32[512,6144]{0,1:T(8,128)}), f32[512,6144]{0,1:T(8,128)}) %all-reduce.5.cloned.1.call-update) | async-done | bytes 12582928 | tf_op jit(solution)/shard_map/psum | solution.py:254
  1236.5 1.9 slice-done
  1238.4 2.4 copy.88
  1240.7 7.8 slice_bitcast_fusion
  1248.5 5.3 copy.89
  1253.8 2.3 slice_bitcast_fusion.1
  (142 shorter events, 24.9 us)
Async XLA Ops:
  7.2 18.6 %copy-start.6 = (f32[512,512]{1,0:T(8,128)S(1)}, f32[512,512]{1,0:T(8,128)}, u32[]{:S(2)}) copy-start(f32[512,512]{1,0:T(8,128)} %param.15) | copy-start | bytes 3145732
  7.2 20.1 %copy-start.27 = (bf16[512,512]{1,0:T(8,128)(2,1)S(1)}, bf16[512,512]{1,0:T(8,128)(2,1)}, u32[]{:S(2)}) copy-start(bf16[512,512]{1,0:T(8,128)(2,1)} %param.22) | copy-start | bytes 1572868
  7.2 80.3 %all-gather.7.cloned.1.call-start = ((), (), s32[]{:S(2)}) async-start(), calls=%async_computation.3 | async-start | bytes 2621440 | tf_op jit(solution)/shard_map/all_gather | solution.py:114
  22.4 4.9 copy-start.29
  22.4 4.9 copy-start.31
  25.0 163.3 %all-gather.9.cloned.1.call-start = ((), (), s32[]{:S(2)}) async-start(), calls=%async_computation.4 | async-start | bytes 7864320 | tf_op jit(solution)/shard_map/all_gather | solution.py:121
  25.7 209.8 %all-gather.15.cloned.1.call-start = ((), (), s32[]{:S(2)}) async-start(), calls=%async_computation.8 | async-start | bytes 2621440 | tf_op jit(solution)/shard_map/all_gather | solution.py:158
  27.3 4.1 copy-start.3
  27.3 314.2 %all-gather.11.cloned.1.call-start = ((), (), s32[]{:S(2)}) async-start(), calls=%async_computation.5 | async-start | bytes 13107200 | tf_op jit(solution)/shard_map/all_gather | solution.py:151
  30.7 357.8 %all-gather.13.cloned.1.call-start = ((), (), s32[]{:S(2)}) async-start(), calls=%async_computation.6 | async-start | bytes 2621440 | tf_op jit(solution)/shard_map/all_gather | solution.py:115
  31.3 497.6 %all-gather.17.cloned.1.call-start = ((), (), s32[]{:S(2)}) async-start(), calls=%async_computation.9 | async-start | bytes 18350080 | tf_op jit(solution)/shard_map/all_gather | solution.py:213
  35.1 920.9 %reduce-scatter.8.cloned.1.call-start = ((), (), s32[]{:S(2)}) async-start(), calls=%async_computation.11 | async-start | bytes 62914560 | tf_op jit(solution)/shard_map/reduce_scatter | solution.py:232
  35.1 46.1 %collective-permute-start = (bf16[512,2048]{1,0:T(8,128)(2,1)S(1)}, bf16[512,2048]{1,0:T(8,128)(2,1)}, u32[]{:S(2)}, u32[]{:S(2)}) collective-permute-start(bf16[512,2048]{1,0:T(8,128)(2,1)S(1)} %copy-done.3), channel_id=1, source_target_pairs={{0,4},{4,0},{8,12},{12,8},{1,5},{5,1},{9,13},{13,9},{2,6},{6,2},{1... | collective-permute-start | bytes 6291464 | tf_op jit(solution)/shard_map/ppermute | solution.py:20
  39.2 149.1 %copy-start.41 = (f32[1536]{0:T(1024)S(1)}, f32[1536]{0:T(1024)}, u32[]{:S(2)}) copy-start(f32[1536]{0:T(1024)} %param.21) | copy-start | bytes 18436
  86.4 302.1 %collective-permute-start.1 = (bf16[1024,2048]{1,0:T(8,128)(2,1)}, bf16[1024,2048]{1,0:T(8,128)(2,1)}, u32[]{:S(2)}, u32[]{:S(2)}) collective-permute-start(bf16[1024,2048]{1,0:T(8,128)(2,1)} %maximum_select_fusion.2), channel_id=1, source_target_pairs={{0,8},{4,12},{8,0},{12,4},{1,9},{5,13},{9,1},{13,5},{2,10},{6,14},... | collective-permute-start | bytes 12582920 | tf_op jit(solution)/shard_map/ppermute | solution.py:20
  208.1 3.9 copy-start.10
  208.1 3.9 copy-start.16
  209.6 3.6 copy-start.14
  212.0 3.0 copy-start.19
  356.2 3.5 copy-start.5
  356.2 3.5 copy-start.11
  356.2 3.5 copy-start.12
  356.2 4.4 copy-start.17
  356.2 4.4 copy-start.24
  356.2 4.4 copy-start.26
  365.1 4.6 copy-start.8
  369.7 5.1 copy-start.18
  369.7 5.1 copy-start.39
  374.8 13.7 %copy-start.42 = (f32[2048]{0:T(1024)S(1)}, f32[2048]{0:T(1024)}, u32[]{:S(2)}) copy-start(f32[2048]{0:T(1024)} %param.25) | copy-start | bytes 24580
  388.5 12.9 %copy-start.40 = (bf16[512,2048]{1,0:T(8,128)(2,1)S(1)}, bf16[512,2048]{1,0:T(8,128)(2,1)}, u32[]{:S(2)}) copy-start(bf16[512,2048]{1,0:T(8,128)(2,1)} %all-gather.13.cloned.1.call-done) | copy-start | bytes 6291460
  401.4 8.6 copy-start.43
  401.4 8.6 copy-start.13
  401.4 8.6 copy-start.45
  410.1 8.3 copy-start
  452.5 650.4 %reduce-scatter.6.cloned.1.call-start = ((), (), s32[]{:S(2)}) async-start(), calls=%async_computation.10 | async-start | bytes 10485760 | tf_op jit(solution)/shard_map/reduce_scatter | solution.py:259
  528.9 6.2 copy-start.44
  546.0 637.6 %reduce-scatter.4.cloned.1.call-start = ((), (), s32[]{:S(2)}) async-start(), calls=%async_computation.7 | async-start | bytes 5242880 | tf_op jit(solution)/shard_map/reduce_scatter | solution.py:155
  560.7 675.8 %all-reduce.5.cloned.1.call-start = ((), (), s32[]{:S(2)}) async-start(), calls=%async_computation.12 | async-start | bytes 25165824 | tf_op jit(solution)/shard_map/psum | solution.py:254
  956.0 148.7 %copy-start.1 = (f32[512,512]{1,0:T(8,128)S(1)}, f32[512,512]{1,0:T(8,128)}, u32[]{:S(2)}) copy-start(f32[512,512]{1,0:T(8,128)} %param.14) | copy-start | bytes 3145732
  956.0 148.7 %copy-start.30 = (f32[512]{0:T(512)S(1)}, f32[512]{0:T(512)}, u32[]{:S(2)}) copy-start(f32[512]{0:T(512)} %copy-done.29) | copy-start | bytes 6148
  956.0 148.7 %copy-start.32 = (f32[512]{0:T(512)S(1)}, f32[512]{0:T(512)}, u32[]{:S(2)}) copy-start(f32[512]{0:T(512)} %copy-done.31) | copy-start | bytes 6148
  956.0 148.7 %copy-start.34 = (f32[512]{0:T(512)S(1)}, f32[512]{0:T(512)}, u32[]{:S(2)}) copy-start(f32[512]{0:T(512)} %param.16) | copy-start | bytes 6148
  956.1 148.7 %copy-start.35 = (f32[512]{0:T(512)S(1)}, f32[512]{0:T(512)}, u32[]{:S(2)}) copy-start(f32[512]{0:T(512)} %param.18) | copy-start | bytes 6148
  956.1 150.9 %copy-start.33 = (f32[512]{0:T(512)S(1)}, f32[512]{0:T(512)}, u32[]{:S(2)}) copy-start(f32[512]{0:T(512)} %get-tuple-element.155) | copy-start | bytes 6148
  956.1 227.5 %copy-start.36 = (f32[512]{0:T(512)S(1)}, f32[512]{0:T(512)}, u32[]{:S(2)}) copy-start(f32[512]{0:T(512)} %param.27) | copy-start | bytes 6148
  956.1 227.5 %copy-start.37 = (f32[512]{0:T(512)S(1)}, f32[512]{0:T(512)}, u32[]{:S(2)}) copy-start(f32[512]{0:T(512)} %param.23) | copy-start | bytes 6148
  957.6 226.0 %copy-start.7 = (f32[512,512]{1,0:T(8,128)S(1)}, f32[512,512]{1,0:T(8,128)}, u32[]{:S(2)}) copy-start(f32[512,512]{1,0:T(8,128)} %param.15) | copy-start | bytes 3145732
  1134.4 121.6 %copy-start.38 = (f32[512]{0:T(512)}, f32[512]{0:T(512)S(1)}, u32[]{:S(2)}) copy-start(f32[512]{0:T(512)S(1)} %get-tuple-element.204) | copy-start | bytes 6148
  (11 other events, 23.6 us)
Sparse Core Ops, SparseCore 0:
  25.1 43.8 all-gather.6
  70.8 117.3 all-gather.8
  189.8 45.6 all-gather.14
  237.8 103.5 all-gather.10
  342.8 45.6 all-gather.12
  390.2 138.6 all-gather.16
  532.0 423.9 reduce-scatter.7
  958.3 144.6 reduce-scatter.5
  1105.9 77.6 reduce-scatter.3
  1185.9 50.5 all-reduce.4
